TPU v7x, 32 devices: a whole 2x2x4 slice. The times are simulated.
32 devices in a mesh: section: 2 (over y), dp: 16 (over z, x, core).
Axes of the slice: x: 2, y: 2, z: 4, core: 2. Of those that a mesh axis runs over, the one named last changes fastest.
Arguments:
- inputs: bfloat16 [32, 128, 1536], P('dp'), parts along dimension 0, may hold values from -6 to 6
- w_query: bfloat16 [2, 1536, 768], P('section'), may hold values from -0.15625 to 0.15625
- w_key: bfloat16 [2, 1536, 768], P('section'), may hold values from -0.15625 to 0.15625
- w_value: bfloat16 [2, 1536, 768], P('section'), may hold values from -0.15625 to 0.15625
- w_out: bfloat16 [2, 768, 1536], P('section'), may hold values from -0.21875 to 0.21875
- mixing: float32 [2], P('section'), may hold values from 0.2 to 0.8
Outputs:
- outputs: bfloat16 [32, 128, 1536], P(('dp', 'section')), parts along dimension 0
There are 16 independent parts, one for each index of `dp`. A program takes and returns all parts, laid end to end along the dimension named above; an argument that names none is the same for every part. Nothing has to cross between parts.
All inputs are finite; a program needn't handle non-finite values.
Results may differ from a plain program's by a relative error of at most 0.023.
Values may be sent and summed in bfloat16 or wider, within the bound.
A program may use at most 128 MiB of HBM per device.

v0:
```python
import functools

import jax
import jax.numpy as jnp
from jax import lax
from jax.experimental import pallas as pl
from jax.experimental.pallas import tpu as pltpu
from jax.sharding import PartitionSpec as P

HEADS = 6

epsilon = 1e-06
score_scale = 0.12
MESH = pl.DeviceIdType.MESH


def norm_rows(tensor):
    return tensor * lax.rsqrt(jnp.mean(tensor * tensor, axis=-1, keepdims=True) + epsilon)


def project(normed, weight):
    return jnp.dot(normed, weight, preferred_element_type=jnp.float32)


def kernel(
    sections,
    inputs_ref,
    wq_hbm,
    wk_hbm,
    wv_hbm,
    wo_hbm,
    mixing_ref,
    out_ref,
    wq,
    wk,
    wv,
    wo,
    h_in,
    h_out,
    v_buf,
    q_buf,
    k_buf,
    val_buf,
    p_buf,
    att_buf,
    acc_buf,
    in_sem,
    wv_sem,
    load_sem,
    hs_sem,
    hr_sem,
    vs_sem,
    vr_sem,
    os_sem,
    or_sem,
):
    me = lax.axis_index("section")
    last = sections - 1
    micro, rows, width = h_in.shape
    features = v_buf.shape[2]
    head = features // HEADS
    chunks = HEADS // 2
    span = features // chunks
    share = micro // sections
    is_first = me == 0
    is_last = me == last
    bf16 = jnp.bfloat16
    f32 = jnp.float32

    def head_part(n):
        return slice(n * head, (n + 1) * head)

    def chunk_part(j):
        return slice(j * span, (j + 1) * span)

    def input_load(i):
        return pltpu.make_async_copy(inputs_ref.at[i], h_in.at[i], in_sem.at[i])

    def value_load(j):
        return pltpu.make_async_copy(
            wv_hbm.at[0, :, chunk_part(j)], wv.at[:, chunk_part(j)], wv_sem.at[j]
        )

    loads = [
        pltpu.make_async_copy(source.at[0], target, load_sem.at[i])
        for i, (source, target) in enumerate(((wq_hbm, wq), (wk_hbm, wk), (wo_hbm, wo)))
    ]

    barrier = pltpu.get_barrier_semaphore()
    for step in range(1, sections):
        pl.semaphore_signal(
            barrier,
            inc=1,
            device_id={"section": lax.rem(me + step, sections)},
            device_id_type=MESH,
        )

    @pl.when(is_first)
    def _():
        input_load(0).start()

    for j in range(chunks):
        value_load(j).start()
    for load in loads:
        load.start()

    @pl.when(is_first)
    def _():
        for i in range(1, micro):
            input_load(i).start()

    pl.semaphore_wait(barrier, sections - 1)

    onward = jnp.minimum(me + 1, last)

    def h_copy(i):
        return pltpu.make_async_remote_copy(
            src_ref=h_out.at[i],
            dst_ref=h_in.at[i],
            send_sem=hs_sem.at[i],
            recv_sem=hr_sem.at[i],
            device_id={"section": onward},
            device_id_type=MESH,
        )

    def v_copy(i, j):
        return pltpu.make_async_remote_copy(
            src_ref=v_buf.at[i, :, chunk_part(j)],
            dst_ref=v_buf.at[i, :, chunk_part(j)],
            send_sem=vs_sem.at[i, j],
            recv_sem=vr_sem.at[i, j],
            device_id={"section": onward},
            device_id_type=MESH,
        )

    def out_copy(i):
        return pltpu.make_async_remote_copy(
            src_ref=h_out.at[i],
            dst_ref=out_ref.at[i % share],
            send_sem=os_sem.at[i],
            recv_sem=or_sem.at[i],
            device_id={"section": i // share},
            device_id_type=MESH,
        )

    row_index = lax.broadcasted_iota(jnp.int32, (rows, rows), 0)
    column_index = lax.broadcasted_iota(jnp.int32, (rows, rows), 1)
    causal = row_index >= column_index

    def fill_probabilities(normed):
        queries = project(normed, wq[...])
        key_rows = project(normed, wk[...])
        for n in range(HEADS):
            q_buf[:, head_part(n)] = norm_rows(queries[:, head_part(n)]).astype(bf16)
            k_buf[:, head_part(n)] = norm_rows(key_rows[:, head_part(n)]).astype(bf16)
        for n in range(HEADS):
            scores = (
                lax.dot_general(
                    q_buf[:, head_part(n)],
                    k_buf[:, head_part(n)],
                    (((1,), (1,)), ((), ())),
                    preferred_element_type=f32,
                )
                * score_scale
            )
            weights = jnp.where(causal, jnp.exp(scores), 0.0)
            p_buf[n] = (weights / jnp.sum(weights, axis=-1, keepdims=True)).astype(bf16)

    @pl.when(is_first)
    def _():
        def one(i, carry):
            input_load(i).wait()
            normed = norm_rows(h_in[i].astype(f32)).astype(bf16)
            for j in range(chunks):

                @pl.when(i == 0)
                def _():
                    value_load(j).wait()

                v_buf[i, :, chunk_part(j)] = project(normed, wv[:, chunk_part(j)]).astype(bf16)
                if sections > 1:

                    @pl.when(i == 0)
                    def _():
                        v_copy(i, j).start()

            @pl.when(i == 0)
            def _():
                for load in loads:
                    load.wait()

            fill_probabilities(normed)
            for n in range(HEADS):
                att_buf[:, head_part(n)] = project(p_buf[n], v_buf[i, :, head_part(n)]).astype(bf16)
            result = (h_in[i].astype(f32) + project(att_buf[...], wo[...])).astype(bf16)
            if sections > 1:
                h_out[i] = result
                h_copy(i).start()

                @pl.when(i > 0)
                def _():
                    for j in range(chunks):
                        v_copy(i, j).start()

            else:
                out_ref[i] = result
            return carry

        lax.fori_loop(0, micro, one, 0)

    if sections > 1:

        @pl.when(jnp.logical_not(is_first))
        def _():
            for j in range(chunks):
                value_load(j).wait()
            for load in loads:
                load.wait()
            mixing = mixing_ref[0]

            def one(i, carry):
                h_copy(i).wait_recv()
                normed = norm_rows(h_in[i].astype(f32)).astype(bf16)
                fill_probabilities(normed)
                val_buf[...] = mixing * project(normed, wv[...])
                for j in range(chunks):
                    v_copy(i, j).wait_recv()
                    if sections > 2:

                        @pl.when(jnp.logical_not(is_last))
                        def _():
                            v_copy(i, j).start()

                    used = (
                        val_buf[:, chunk_part(j)]
                        + (1.0 - mixing) * v_buf[i, :, chunk_part(j)].astype(f32)
                    ).astype(bf16)
                    for n in range(2):
                        att_buf[:, head_part(2 * j + n)] = project(
                            p_buf[2 * j + n], used[:, head_part(n)]
                        ).astype(bf16)
                    term = project(att_buf[:, chunk_part(j)], wo[chunk_part(j), :])
                    if j == 0:
                        acc_buf[...] = term
                    elif j < chunks - 1:
                        acc_buf[...] += term
                result = (h_in[i].astype(f32) + (acc_buf[...] + term)).astype(bf16)
                mine = jnp.logical_and(is_last, i // share == last)

                @pl.when(mine)
                def _():
                    out_ref[i % share] = result

                @pl.when(jnp.logical_not(mine))
                def _():
                    h_out[i] = result

                    @pl.when(is_last)
                    def _():
                        out_copy(i).start()

                    if sections > 2:

                        @pl.when(jnp.logical_not(is_last))
                        def _():
                            h_copy(i).start()

                return carry

            lax.fori_loop(0, micro, one, 0)

    @pl.when(jnp.logical_not(is_last))
    def _():
        for i in range(micro):
            for j in range(chunks):
                v_copy(i, j).wait_send()
            h_copy(i).wait_send()

    for i in range(micro):
        if i // share != last:

            @pl.when(is_last)
            def _():
                out_copy(i).wait_send()

            @pl.when(me == i // share)
            def _():
                out_copy(i).wait_recv()


def body(inputs, w_query, w_key, w_value, w_out, mixing):
    sections = lax.axis_size("section")
    micro, rows, width = inputs.shape
    features = w_value.shape[2]
    share = micro // sections
    bf16 = jnp.bfloat16
    anywhere = pl.BlockSpec(memory_space=pltpu.HBM)
    dma = pltpu.SemaphoreType.DMA
    return pl.pallas_call(
        functools.partial(kernel, sections),
        out_shape=pltpu.VMEM((share, rows, width), bf16),
        in_specs=[anywhere] * 5 + [pl.BlockSpec(memory_space=pltpu.SMEM)],
        out_specs=pl.BlockSpec(memory_space=pltpu.VMEM),
        scratch_shapes=[
            pltpu.VMEM((width, features), bf16),
            pltpu.VMEM((width, features), bf16),
            pltpu.VMEM((width, features), bf16),
            pltpu.VMEM((features, width), bf16),
            pltpu.VMEM((micro, rows, width), bf16),
            pltpu.VMEM((micro, rows, width), bf16),
            pltpu.VMEM((micro, rows, features), bf16),
            pltpu.VMEM((rows, features), bf16),
            pltpu.VMEM((rows, features), bf16),
            pltpu.VMEM((rows, features), jnp.float32),
            pltpu.VMEM((HEADS, rows, rows), bf16),
            pltpu.VMEM((rows, features), bf16),
            pltpu.VMEM((rows, width), jnp.float32),
            dma((micro,)),
            dma((HEADS // 2,)),
            dma((3,)),
            dma((micro,)),
            dma((micro,)),
            dma((micro, HEADS // 2)),
            dma((micro, HEADS // 2)),
            dma((micro,)),
            dma((micro,)),
        ],
        compiler_params=pltpu.CompilerParams(
            collective_id=0, has_side_effects=True, vmem_limit_bytes=62 * 1024 * 1024
        ),
        name="sections",
    )(inputs, w_query, w_key, w_value, w_out, mixing)


def solution(mesh):
    in_specs = (
        P("dp", None, None),
        P("section", None, None),
        P("section", None, None),
        P("section", None, None),
        P("section", None, None),
        P("section"),
    )
    out_specs = P(("dp", "section"), None, None)
    return jax.shard_map(body, mesh=mesh, in_specs=in_specs, out_specs=out_specs, check_vma=False)
```

profile of v0, /device:TPU:28, one launch (start us, length us, event | category | flops | bytes accessed | tf_op | source)
XLA Modules:
  0.0 31.2 jit_solution(6874963254912575823)
XLA Ops:
  0.7 29.7 %sections.1 = bf16[1,128,1536]{2,1,0:T(8,128)(2,1)S(1)} custom-call(bf16[2,128,1536]{2,1,0:T(8,128)(2,1)} %inputs_ref.1, bf16[1,1536,768]{2,1,0:T(8,128)(2,1)} %wq_hbm.1, bf16[1,1536,768]{2,1,0:T(8,128)(2,1)} %wk_hbm.1, bf16[1,1536,768]{2,1,0:T(8,128)(2,1)} %wv_hbm.1, bf16[1,768,1536]{2,1,0:T(8,128)(2,1)} %wo_hbm.1, f32[1]{0:T(128)S(6)} %copy.9.mixing_ref), custom_call_target="tpu_custom_call" | custom-call | tf_op jit(solution)/shard_map/sections/pallas_call | solution.py:299
  30.4 0.7 %copy.8 = bf16[1,128,1536]{2,1,0:T(8,128)(2,1)} copy(bf16[1,128,1536]{2,1,0:T(8,128)(2,1)S(1)} %sections.1) | data formatting | bytes 786432
where the time goes:
time: 31.7 us; the launch traced here: 31.2 us
  Pallas kernels  29.7 us (94%)
  local copies, waits for them, and re-layouts  0.75 us (2%)
  between operations  0.66 us (2%)
    pallas_call x1, Pallas kernels, body(): pl.pallas_call(functools.partial(kernel, sections), out_shape=pltpu.VMEM(...  29.7 us
    unnamed x1, local copies, waits for them, and re-layouts  0.75 us

commit v1 on v0

--- a/solution.py
+++ b/solution.py
@@ -332,6 +332,404 @@
     )(inputs, w_query, w_key, w_value, w_out, mixing)
 
 
+def pair_kernel(
+    inputs_ref,
+    wq_hbm,
+    wk_hbm,
+    wv_hbm,
+    wo_hbm,
+    mixing_ref,
+    out_ref,
+    wq,
+    wk,
+    wv,
+    wo,
+    wx,
+    h_in,
+    h_out,
+    normed_buf,
+    v_buf,
+    q_buf,
+    k_buf,
+    used_buf,
+    p_buf,
+    ps_buf,
+    pv_buf,
+    att_buf,
+    q_acc,
+    k_acc,
+    v_acc,
+    out_acc,
+    in_sem,
+    wv_sem,
+    load_sem,
+    hs_sem,
+    hr_sem,
+    cs_sem,
+    cr_sem,
+    vs_sem,
+    vr_sem,
+    ps_sem,
+    pr_sem,
+    ys_sem,
+    yr_sem,
+    xs_sem,
+    xr_sem,
+    ds_sem,
+    dr_sem,
+):
+    me = lax.axis_index("section")
+    dp = lax.axis_index("dp")
+    across = dp + 2 - 4 * ((dp // 2) % 2)
+    beside = dp + 1 - 2 * (dp % 2)
+    quarter = dp % 4
+    far_quarter = quarter + 2 - 4 * (quarter // 2)
+    beside_quarters = beside % 4, far_quarter + 1 - 2 * (quarter % 2)
+    micro, rows, width = h_in.shape
+    features = wv.shape[1]
+    head = features // HEADS
+    chunks = HEADS // 2
+    span = features // chunks
+    cuts = cr_sem.shape[0]
+    cut = width // cuts
+    halves = hr_sem.shape[0]
+    half = rows // halves
+    pieces = yr_sem.shape[0]
+    piece = features // (4 * pieces)
+    bf16 = jnp.bfloat16
+    f32 = jnp.float32
+
+    def head_part(n):
+        return slice(n * head, (n + 1) * head)
+
+    def chunk_part(j):
+        return slice(j * span, (j + 1) * span)
+
+    def cut_part(c):
+        return slice(c * cut, (c + 1) * cut)
+
+    def half_part(t):
+        return slice(t * half, (t + 1) * half)
+
+    def input_load(i):
+        return pltpu.make_async_copy(inputs_ref.at[i], h_in.at[i], in_sem.at[i])
+
+    def value_load(j):
+        return pltpu.make_async_copy(
+            wv_hbm.at[0, :, chunk_part(j)], wv.at[:, chunk_part(j)], wv_sem.at[j]
+        )
+
+    query_load, key_load, out_load = (
+        pltpu.make_async_copy(source.at[0], target, load_sem.at[i])
+        for i, (source, target) in enumerate(((wq_hbm, wq), (wk_hbm, wk), (wo_hbm, wo)))
+    )
+
+    def send(source, target, send_sem, recv_sem, device):
+        return pltpu.make_async_remote_copy(
+            src_ref=source,
+            dst_ref=target,
+            send_sem=send_sem,
+            recv_sem=recv_sem,
+            device_id=device,
+            device_id_type=MESH,
+        )
+
+    def half_copy(t):
+        return send(
+            h_out.at[0, half_part(t), :],
+            h_in.at[0, half_part(t), :],
+            hs_sem.at[t],
+            hr_sem.at[t],
+            {"section": 1},
+        )
+
+    def cut_copy(c):
+        return send(
+            h_out.at[1, :, cut_part(c)],
+            h_in.at[1, :, cut_part(c)],
+            cs_sem.at[c],
+            cr_sem.at[c],
+            {"section": 1},
+        )
+
+    def v_copy(j):
+        part = v_buf.at[1, :, chunk_part(j)]
+        return send(part, part, vs_sem.at[j], vr_sem.at[j], {"section": 1})
+
+    def p_copy(t):
+        part = ps_buf.at[:, half_part(t), :]
+        return send(part, part, ps_sem.at[0, t], pr_sem.at[0, t], {"section": 0})
+
+    def pv_copy(t):
+        part = pv_buf.at[half_part(t), :]
+        return send(part, part, ps_sem.at[1, t], pr_sem.at[1, t], {"section": 0})
+
+    def piece_part(owner, i):
+        return pl.ds(pl.multiple_of((owner * pieces + i) * piece, piece), piece)
+
+    def y_copy(i):
+        part = piece_part(quarter, i)
+        return send(wo.at[part, :], wx.at[part, :], ys_sem.at[i], yr_sem.at[i], {"section": 0})
+
+    def x_copy(owner, i):
+        part = wx.at[piece_part(owner, i), :]
+        return send(part, part, xs_sem.at[i], xr_sem.at[i], {"dp": across})
+
+    def core_copy(far, owner, i):
+        part = wx.at[piece_part(owner, i), :]
+        return send(part, part, ds_sem.at[far, i], dr_sem.at[far, i], {"dp": beside})
+
+    barrier = pltpu.get_barrier_semaphore()
+    for device in ({"section": 1 - me}, {"dp": across}, {"dp": beside}):
+        pl.semaphore_signal(barrier, inc=1, device_id=device, device_id_type=MESH)
+
+    row_index = lax.broadcasted_iota(jnp.int32, (rows, rows), 0)
+    column_index = lax.broadcasted_iota(jnp.int32, (rows, rows), 1)
+    causal = row_index >= column_index
+
+    def scores_of(part, keys, n):
+        return (
+            lax.dot_general(
+                q_buf[part, head_part(n)],
+                k_buf[:keys, head_part(n)],
+                (((1,), (1,)), ((), ())),
+                preferred_element_type=f32,
+            )
+            * score_scale
+        )
+
+    def fill_probabilities():
+        for n in range(HEADS):
+            weights = jnp.where(causal, jnp.exp(scores_of(slice(0, rows), rows, n)), 0.0)
+            p_buf[n] = (weights / jnp.sum(weights, axis=-1, keepdims=True)).astype(bf16)
+
+    def fill_heads(target, part, values):
+        for n in range(HEADS):
+            target[part, head_part(n)] = norm_rows(values[:, head_part(n)]).astype(bf16)
+
+    @pl.when(me == 0)
+    def _():
+        for i in range(micro):
+            input_load(i).start()
+        for j in range(chunks):
+            value_load(j).start()
+        query_load.start()
+        key_load.start()
+        out_load.start()
+        for i in range(micro):
+            input_load(i).wait()
+            normed_buf[i * rows : (i + 1) * rows, :] = norm_rows(h_in[i].astype(f32)).astype(bf16)
+        pl.semaphore_wait(barrier, 3)
+        for j in range(chunks):
+            value_load(j).wait()
+            values = project(normed_buf[...], wv[:, chunk_part(j)]).astype(bf16)
+            v_buf[1, :, chunk_part(j)] = values[rows:, :]
+            if j < chunks - 1:
+                v_copy(j).start()
+            v_buf[0, :, chunk_part(j)] = values[:rows, :]
+
+        def attend(i):
+            part = slice(i * rows, (i + 1) * rows)
+            if i == 0:
+                query_load.wait()
+            fill_heads(q_buf, slice(0, rows), project(normed_buf[part, :], wq[...]))
+            if i == 0:
+                key_load.wait()
+            fill_heads(k_buf, slice(0, rows), project(normed_buf[part, :], wk[...]))
+            fill_probabilities()
+            for n in range(HEADS):
+                att_buf[:, head_part(n)] = project(p_buf[n], v_buf[i, :, head_part(n)]).astype(bf16)
+
+        def pass_on(i):
+            y_copy(i).wait_recv()
+            x_copy(quarter, i).start()
+            core_copy(0, quarter, i).start()
+
+        def pass_far(i):
+            x_copy(far_quarter, i).wait_recv()
+            core_copy(1, far_quarter, i).start()
+
+        attend(0)
+        out_load.wait()
+        for t in range(halves):
+            h_out[0, half_part(t), :] = (
+                h_in[0, half_part(t), :].astype(f32) + project(att_buf[half_part(t), :], wo[...])
+            ).astype(bf16)
+            half_copy(t).start()
+        pass_on(0)
+        attend(1)
+        pass_on(1)
+        for c in range(cuts):
+            h_out[1, :, cut_part(c)] = (
+                h_in[1, :, cut_part(c)].astype(f32) + project(att_buf[...], wo[:, cut_part(c)])
+            ).astype(bf16)
+            cut_copy(c).start()
+        v_copy(chunks - 1).start()
+        for i in range(2, pieces):
+            pass_on(i)
+            pass_far(i - 2)
+        for i in range(pieces - 2, pieces):
+            pass_far(i)
+        for far in range(2):
+            for i in range(pieces):
+                core_copy(far, beside_quarters[far], i).wait_recv()
+        for t in range(halves):
+            keys = (t + 1) * half
+            p_copy(t).wait_recv()
+            pv_copy(t).wait_recv()
+            for n in range(HEADS):
+                att_buf[half_part(t), head_part(n)] = (
+                    pv_buf[half_part(t), head_part(n)].astype(f32)
+                    + project(ps_buf[n, half_part(t), :keys], v_buf[0, :keys, head_part(n)])
+                ).astype(bf16)
+            out_ref[0, half_part(t), :] = (
+                h_out[0, half_part(t), :].astype(f32) + project(att_buf[half_part(t), :], wx[...])
+            ).astype(bf16)
+        for t in range(halves):
+            half_copy(t).wait_send()
+        for c in range(cuts):
+            cut_copy(c).wait_send()
+        for j in range(chunks):
+            v_copy(j).wait_send()
+        for i in range(pieces):
+            x_copy(quarter, i).wait_send()
+            core_copy(0, quarter, i).wait_send()
+            core_copy(1, far_quarter, i).wait_send()
+
+    @pl.when(me == 1)
+    def _():
+        out_load.start()
+        query_load.start()
+        key_load.start()
+        for j in range(chunks):
+            value_load(j).start()
+        mixing = mixing_ref[0]
+        ps_buf[...] = jnp.zeros_like(ps_buf)
+        out_load.wait()
+        pl.semaphore_wait(barrier, 3)
+        for i in range(pieces):
+            y_copy(i).start()
+        query_load.wait()
+        key_load.wait()
+        for j in range(chunks):
+            value_load(j).wait()
+        for t in range(halves):
+            part = half_part(t)
+            keys = (t + 1) * half
+            half_copy(t).wait_recv()
+            normed = norm_rows(h_in[0, part, :].astype(f32)).astype(bf16)
+            fill_heads(q_buf, part, project(normed, wq[...]))
+            fill_heads(k_buf, part, project(normed, wk[...]))
+            used_buf[part, :] = (mixing * project(normed, wv[...])).astype(bf16)
+            for n in range(HEADS):
+                weights = jnp.where(causal[part, :keys], jnp.exp(scores_of(part, keys, n)), 0.0)
+                share = weights / jnp.sum(weights, axis=-1, keepdims=True)
+                ps_buf[n, part, :keys] = ((1.0 - mixing) * share).astype(bf16)
+                pv_buf[part, head_part(n)] = project(
+                    share.astype(bf16), used_buf[:keys, head_part(n)]
+                ).astype(bf16)
+            p_copy(t).start()
+            pv_copy(t).start()
+        squares = jnp.zeros((rows, 1), f32)
+        for c in range(cuts):
+            cut_copy(c).wait_recv()
+            piece_in = h_in[1, :, cut_part(c)]
+            for target, weight in ((q_acc, wq), (k_acc, wk), (v_acc, wv)):
+                term = project(piece_in, weight[cut_part(c), :])
+                if c == 0:
+                    target[...] = term
+                else:
+                    target[...] += term
+            wide = piece_in.astype(f32)
+            squares += jnp.sum(wide * wide, axis=-1, keepdims=True)
+        scale = lax.rsqrt(squares / width + epsilon)
+        fill_heads(q_buf, slice(0, rows), q_acc[...] * scale)
+        fill_heads(k_buf, slice(0, rows), k_acc[...] * scale)
+        fill_probabilities()
+        for j in range(chunks):
+            v_copy(j).wait_recv()
+            used = (
+                mixing * (v_acc[:, chunk_part(j)] * scale)
+                + (1.0 - mixing) * v_buf[1, :, chunk_part(j)].astype(f32)
+            ).astype(bf16)
+            for n in range(2):
+                att_buf[:, head_part(2 * j + n)] = project(
+                    p_buf[2 * j + n], used[:, head_part(n)]
+                ).astype(bf16)
+            term = project(att_buf[:, chunk_part(j)], wo[chunk_part(j), :])
+            if j == 0:
+                out_acc[...] = term
+            elif j < chunks - 1:
+                out_acc[...] += term
+        out_ref[0] = (h_in[1].astype(f32) + (out_acc[...] + term)).astype(bf16)
+        for i in range(pieces):
+            y_copy(i).wait_send()
+        for t in range(halves):
+            p_copy(t).wait_send()
+            pv_copy(t).wait_send()
+
+
+def pair_body(inputs, w_query, w_key, w_value, w_out, mixing):
+    micro, rows, width = inputs.shape
+    features = w_value.shape[2]
+    head = features // HEADS
+    chunks = HEADS // 2
+    halves, cuts, pieces = 2, 6, 6
+    bf16 = jnp.bfloat16
+    f32 = jnp.float32
+    anywhere = pl.BlockSpec(memory_space=pltpu.HBM)
+    dma = pltpu.SemaphoreType.DMA
+    return pl.pallas_call(
+        pair_kernel,
+        out_shape=pltpu.VMEM((1, rows, width), bf16),
+        in_specs=[anywhere] * 5 + [pl.BlockSpec(memory_space=pltpu.SMEM)],
+        out_specs=pl.BlockSpec(memory_space=pltpu.VMEM),
+        scratch_shapes=[
+            pltpu.VMEM((width, features), bf16),
+            pltpu.VMEM((width, features), bf16),
+            pltpu.VMEM((width, features), bf16),
+            pltpu.VMEM((features, width), bf16),
+            pltpu.VMEM((features, width), bf16),
+            pltpu.VMEM((micro, rows, width), bf16),
+            pltpu.VMEM((micro, rows, width), bf16),
+            pltpu.VMEM((micro * rows, width), bf16),
+            pltpu.VMEM((micro, rows, features), bf16),
+            pltpu.VMEM((rows, features), bf16),
+            pltpu.VMEM((rows, features), bf16),
+            pltpu.VMEM((rows, features), bf16),
+            pltpu.VMEM((HEADS, rows, rows), bf16),
+            pltpu.VMEM((HEADS, rows, rows), bf16),
+            pltpu.VMEM((rows, features), bf16),
+            pltpu.VMEM((rows, features), bf16),
+            pltpu.VMEM((rows, features), f32),
+            pltpu.VMEM((rows, features), f32),
+            pltpu.VMEM((rows, features), f32),
+            pltpu.VMEM((rows, width), f32),
+            dma((micro,)),
+            dma((chunks,)),
+            dma((3,)),
+            dma((halves,)),
+            dma((halves,)),
+            dma((cuts,)),
+            dma((cuts,)),
+            dma((chunks,)),
+            dma((chunks,)),
+            dma((2, halves)),
+            dma((2, halves)),
+            dma((pieces,)),
+            dma((pieces,)),
+            dma((pieces,)),
+            dma((pieces,)),
+            dma((2, pieces)),
+            dma((2, pieces)),
+        ],
+        compiler_params=pltpu.CompilerParams(
+            collective_id=0, has_side_effects=True, vmem_limit_bytes=62 * 1024 * 1024
+        ),
+        name="section_pair",
+    )(inputs, w_query, w_key, w_value, w_out, mixing)
+
+
 def solution(mesh):
     in_specs = (
         P("dp", None, None),
@@ -342,4 +740,10 @@
         P("section"),
     )
     out_specs = P(("dp", "section"), None, None)
-    return jax.shard_map(body, mesh=mesh, in_specs=in_specs, out_specs=out_specs, check_vma=False)
+    paired = mesh.shape["section"] == 2 and mesh.shape["dp"] % 4 == 0
+
+    def either(inputs, *weights):
+        chosen = pair_body if paired and inputs.shape[0] == 2 else body
+        return chosen(inputs, *weights)
+
+    return jax.shard_map(either, mesh=mesh, in_specs=in_specs, out_specs=out_specs, check_vma=False)

time: 31.7 us -> 30.1 us (0.950); the launches traced: 31.2 us -> 29.9 us
  Pallas kernels: 29.7 us -> 28.5 us
    pallas_call x1, Pallas kernels: 29.7 us -> 28.5 us  [pair_body(): pl.pallas_call(pair_kernel, out_shape=pltpu.VMEM((1, rows, width), bf16),...]
where the time goes in v1:
time: 30.1 us; the launch traced here: 29.9 us
  Pallas kernels  28.5 us (95%)
  local copies, waits for them, and re-layouts  0.75 us (2%)
  between operations  0.66 us (2%)
    pallas_call x1, Pallas kernels, pair_body(): pl.pallas_call(pair_kernel, out_shape=pltpu.VMEM((1, rows, width), bf16),...  28.5 us
    unnamed x1, local copies, waits for them, and re-layouts  0.75 us

profile of v1, /device:TPU:28, one launch (start us, length us, event | category | flops | bytes accessed | tf_op | source)
XLA Modules:
  0.0 29.9 jit_solution(4073212020616230076)
XLA Ops:
  0.7 28.5 %section_pair.1 = bf16[1,128,1536]{2,1,0:T(8,128)(2,1)S(1)} custom-call(bf16[2,128,1536]{2,1,0:T(8,128)(2,1)} %inputs_ref.1, bf16[1,1536,768]{2,1,0:T(8,128)(2,1)} %wq_hbm.1, bf16[1,1536,768]{2,1,0:T(8,128)(2,1)} %wk_hbm.1, bf16[1,1536,768]{2,1,0:T(8,128)(2,1)} %wv_hbm.1, bf16[1,768,1536]{2,1,0:T(8,128)(2,1)} %wo_hbm.1, f32[1]{0:T(128)S(6)} %copy.9.mixing_ref), custom_call_target="tpu_custom_call" | custom-call | tf_op jit(solution)/shard_map/section_pair/pallas_call | solution.py:682
  29.2 0.7 %copy.8 = bf16[1,128,1536]{2,1,0:T(8,128)(2,1)} copy(bf16[1,128,1536]{2,1,0:T(8,128)(2,1)S(1)} %section_pair.1) | data formatting | bytes 786432

commit v2 on v0

--- a/solution.py
+++ b/solution.py
@@ -8,6 +8,8 @@
 from jax.sharding import PartitionSpec as P
 
 HEADS = 6
+CUTS = 6
+PIECES = 4
 
 epsilon = 1e-06
 score_scale = 0.12
@@ -332,6 +334,465 @@
     )(inputs, w_query, w_key, w_value, w_out, mixing)
 
 
+def pair_kernel(
+    inputs_ref,
+    wq_hbm,
+    wk_hbm,
+    wv_hbm,
+    wo_hbm,
+    mixing_ref,
+    out_ref,
+    wq,
+    wk,
+    wv,
+    wo,
+    wx,
+    h_in,
+    h_out,
+    normed_buf,
+    v_buf,
+    q_buf,
+    k_buf,
+    used_buf,
+    p_buf,
+    low_buf,
+    high_buf,
+    att_buf,
+    q_acc,
+    k_acc,
+    v_acc,
+    val_buf,
+    out_acc,
+    load_sem,
+    send_sem,
+    recv_sem,
+    met_sem,
+):
+    me = lax.axis_index("section")
+    dp = lax.axis_index("dp")
+    core = dp % 2
+    across = dp + 2 - 4 * ((dp // 2) % 2)
+    along = dp + 4 - 8 * ((dp // 4) % 2)
+    beside = dp + 1 - 2 * core
+    quarter = (dp // 2 + dp // 4) % 2 * 2 + core
+    far_quarter = quarter + 2 - 4 * (quarter // 2)
+    micro, rows, width = h_in.shape
+    features = wv.shape[1]
+    head = features // HEADS
+    chunks = HEADS // 2
+    span = features // chunks
+    half = rows // 2
+    cut = width // CUTS
+    share = features // 4
+    piece = share // PIECES
+    bf16 = jnp.bfloat16
+    f32 = jnp.float32
+    everything = slice(0, rows)
+    early = slice(0, (chunks - 1) * span)
+    late = slice((chunks - 1) * span, features)
+
+    def head_part(n):
+        return slice(n * head, (n + 1) * head)
+
+    def chunk_part(j):
+        return slice(j * span, (j + 1) * span)
+
+    def cut_part(c):
+        return slice(c * cut, (c + 1) * cut)
+
+    def half_part(t):
+        return slice(t * half, (t + 1) * half)
+
+    def sequence_part(i):
+        return slice(i * rows, (i + 1) * rows)
+
+    def load(source, target, n):
+        return pltpu.make_async_copy(source, target, load_sem.at[n])
+
+    def input_load(i):
+        return load(inputs_ref.at[i], h_in.at[i], i)
+
+    def value_load(j):
+        return load(wv_hbm.at[0, :, chunk_part(j)], wv.at[:, chunk_part(j)], 2 + j)
+
+    query_load = load(wq_hbm.at[0], wq, 5)
+    key_load = load(wk_hbm.at[0], wk, 6)
+    out_load = load(wo_hbm.at[0], wo, 7)
+    values_load = load(wv_hbm.at[0], wv, 2)
+    rest_load = load(wo_hbm.at[0, : 3 * share, :], wo.at[: 3 * share, :], 1)
+
+    def share_load(r):
+        part = pl.ds(pl.multiple_of((quarter + r) % 4 * share, share), share)
+        return load(wo_hbm.at[0, part, :], wo.at[part, :], min(r, 1))
+
+    def send(source, target, sent, received, device):
+        return pltpu.make_async_remote_copy(
+            src_ref=source,
+            dst_ref=target,
+            send_sem=send_sem.at[sent],
+            recv_sem=recv_sem.at[received],
+            device_id=device,
+            device_id_type=MESH,
+        )
+
+    def half_copy(i, t):
+        part = (i, half_part(t))
+        return send(h_out.at[part], h_in.at[part], 0, 2 * i + t, {"section": 1})
+
+    def cut_copy(c):
+        part = (1, half_part(1), cut_part(c))
+        return send(h_out.at[part], h_in.at[part], 0, 3 + c, {"section": 1})
+
+    def v_copy(part, n):
+        return send(v_buf.at[1, :, part], v_buf.at[1, :, part], 1, 3 + CUTS + n, {"section": 1})
+
+    def low_copy():
+        return send(low_buf, low_buf, 2, 0, {"section": 0})
+
+    def high_copy(g):
+        return send(high_buf.at[g], high_buf.at[g], 3, 1 + g, {"section": 0})
+
+    def piece_part(owner, i):
+        return pl.ds(pl.multiple_of(owner * share + i * piece, piece), piece)
+
+    def y_copy(i):
+        part = piece_part(quarter, i)
+        return send(wo.at[part, :], wx.at[part, :], min(i, 1), 3 + i, {"section": 0})
+
+    def side_copy(owner, i):
+        part = wx.at[piece_part(owner, i), :]
+        return send(part, part, 2, 3 + PIECES + i, {"dp": along if i % 2 else across})
+
+    def core_copy(owner, i):
+        part = wx.at[piece_part(owner, i), :]
+        return send(part, part, 3, 3 + 2 * PIECES, {"dp": beside})
+
+    def rows_wait(count, sent, received):
+        part = wx.at[:count, :]
+        return send(part, part, sent, received, {"dp": beside})
+
+    barrier = pltpu.get_barrier_semaphore()
+
+    @pl.when(me == 1)
+    def _():
+        share_load(0).start()
+        pl.semaphore_wait(barrier, 1)
+        pl.semaphore_signal(met_sem, inc=1, device_id={"section": 0}, device_id_type=MESH)
+
+    @pl.when(me == 0)
+    def _():
+        for device in ({"section": 1}, {"dp": across}, {"dp": along}, {"dp": beside}):
+            pl.semaphore_signal(barrier, inc=1, device_id=device, device_id_type=MESH)
+
+    row_index = lax.broadcasted_iota(jnp.int32, (rows, rows), 0)
+    column_index = lax.broadcasted_iota(jnp.int32, (rows, rows), 1)
+    causal = row_index >= column_index
+
+    def normed_rows(values):
+        return norm_rows(values.astype(f32)).astype(bf16)
+
+    def fill_heads(target, part, values):
+        for n in range(HEADS):
+            target[part, head_part(n)] = norm_rows(values[:, head_part(n)]).astype(bf16)
+
+    def probabilities(part, keys, n):
+        scores = (
+            lax.dot_general(
+                q_buf[part, head_part(n)],
+                k_buf[:keys, head_part(n)],
+                (((1,), (1,)), ((), ())),
+                preferred_element_type=f32,
+            )
+            * score_scale
+        )
+        weights = jnp.where(causal[part, :keys], jnp.exp(scores), 0.0)
+        return weights / jnp.sum(weights, axis=-1, keepdims=True)
+
+    @pl.when(me == 0)
+    def _():
+        input_load(1).start()
+        value_load(0).start()
+        input_load(0).start()
+        for j in range(1, chunks):
+            value_load(j).start()
+
+        def fill_normed(i):
+            with jax.named_scope(f"in{i}"):
+                input_load(i).wait()
+            normed_buf[sequence_part(i), :] = normed_rows(h_in[i])
+
+        def fill_values(i, j):
+            v_buf[i, :, chunk_part(j)] = project(
+                normed_buf[sequence_part(i), :], wv[:, chunk_part(j)]
+            ).astype(bf16)
+
+        fill_normed(1)
+        query_load.start()
+        key_load.start()
+        out_load.start()
+        for j in range(chunks):
+            with jax.named_scope(f"wv{j}"):
+                value_load(j).wait()
+            fill_values(1, j)
+            if j == 0:
+                with jax.named_scope("met"):
+                    pl.semaphore_wait(met_sem, 1)
+            if j < chunks - 1:
+                v_copy(chunk_part(j), 0).start()
+            else:
+
+                @pl.when(core == 0)
+                def _():
+                    v_copy(late, 1).start()
+
+        fill_normed(0)
+        for j in range(chunks):
+            fill_values(0, j)
+
+        def attend(i):
+            normed = normed_buf[sequence_part(i), :]
+            if i == 0:
+                with jax.named_scope("wq"):
+                    query_load.wait()
+            fill_heads(q_buf, everything, project(normed, wq[...]))
+            if i == 0:
+                with jax.named_scope("wk"):
+                    key_load.wait()
+            fill_heads(k_buf, everything, project(normed, wk[...]))
+            for n in range(HEADS):
+                p_buf[n] = probabilities(everything, rows, n).astype(bf16)
+            for n in range(HEADS):
+                att_buf[:, head_part(n)] = project(p_buf[n], v_buf[i, :, head_part(n)]).astype(bf16)
+
+        def next_rows(i, part, columns):
+            h_out[i, part, columns] = (
+                h_in[i, part, columns].astype(f32) + project(att_buf[part, :], wo[:, columns])
+            ).astype(bf16)
+
+        def pass_on(i):
+            with jax.named_scope(f"pass{i}"):
+                y_copy(i).wait_recv()
+            side_copy(quarter, i).start()
+            core_copy(quarter, i).start()
+
+        def pass_far(i):
+            with jax.named_scope(f"far{i}"):
+                side_copy(far_quarter, i).wait_recv()
+            core_copy(far_quarter, i).start()
+
+        attend(0)
+        with jax.named_scope("wo"):
+            out_load.wait()
+        for t in range(2):
+            with jax.named_scope(f"h0{t}"):
+                next_rows(0, half_part(t), slice(0, width))
+                half_copy(0, t).start()
+        with jax.named_scope("bar"):
+            pl.semaphore_wait(barrier, 3)
+        pass_on(0)
+        attend(1)
+        with jax.named_scope("h1"):
+            next_rows(1, half_part(0), slice(0, width))
+            half_copy(1, 0).start()
+            for c in range(CUTS):
+                next_rows(1, half_part(1), cut_part(c))
+                cut_copy(c).start()
+
+        @pl.when(core == 1)
+        def _():
+            v_copy(late, 1).start()
+
+        for i in range(1, PIECES):
+            pass_on(i)
+            pass_far(i - 1)
+        pass_far(PIECES - 1)
+        with jax.named_scope("core"):
+            rows_wait(2 * share, 3, 3 + 2 * PIECES).wait_recv()
+        for t in range(2):
+            part = half_part(t)
+            keys = (t + 1) * half
+            for n in range(HEADS):
+                group, place = n // chunks, n % chunks
+                if t == 0:
+                    if n == 0:
+                        with jax.named_scope("low"):
+                            low_copy().wait_recv()
+                    passed = low_buf[n // 2, :, n % 2 * half : (n % 2 + 1) * half]
+                    own = low_buf[chunks + n]
+                else:
+                    if place == 0:
+                        with jax.named_scope(f"high{group}"):
+                            high_copy(group).wait_recv()
+                    passed = high_buf[group, place]
+                    own = high_buf[group, chunks + place]
+                att_buf[part, head_part(n)] = (
+                    own.astype(f32) + project(passed, v_buf[0, :keys, head_part(n)])
+                ).astype(bf16)
+            out_ref[0, part, :] = (
+                h_out[0, part, :].astype(f32) + project(att_buf[part, :], wx[...])
+            ).astype(bf16)
+        with jax.named_scope("end"):
+            send(h_out, h_in, 0, 0, {"section": 1}).wait_send()
+            send(v_buf.at[1], v_buf.at[1], 1, 0, {"section": 1}).wait_send()
+            rows_wait(share, 2, 0).wait_send()
+            rows_wait(2 * share, 3, 0).wait_send()
+
+    @pl.when(me == 1)
+    def _():
+        mixing = mixing_ref[0]
+        with jax.named_scope("wo"):
+            share_load(0).wait()
+        for i in range(PIECES):
+            y_copy(i).start()
+        with jax.named_scope("y0"):
+            rows_wait(piece, 0, 0).wait_send()
+        query_load.start()
+        key_load.start()
+        values_load.start()
+        for r in range(1, 4):
+            share_load(r).start()
+        with jax.named_scope("loads"):
+            query_load.wait()
+            key_load.wait()
+            values_load.wait()
+            rest_load.wait()
+
+        def fill_rows(i, t):
+            part = half_part(t)
+            with jax.named_scope(f"half{i}{t}"):
+                half_copy(i, t).wait_recv()
+            normed = normed_rows(h_in[i, part, :])
+            fill_heads(q_buf, part, project(normed, wq[...]))
+            fill_heads(k_buf, part, project(normed, wk[...]))
+            return mixing * project(normed, wv[...])
+
+        for t in range(2):
+            part = half_part(t)
+            keys = (t + 1) * half
+            used_buf[part, :] = fill_rows(0, t).astype(bf16)
+            for n in range(HEADS):
+                group, place = n // chunks, n % chunks
+                shares = probabilities(part, keys, n)
+                passed = ((1.0 - mixing) * shares).astype(bf16)
+                own = project(shares.astype(bf16), used_buf[:keys, head_part(n)]).astype(bf16)
+                if t == 0:
+                    low_buf[n // 2, :, n % 2 * half : (n % 2 + 1) * half] = passed
+                    low_buf[chunks + n] = own
+                else:
+                    high_buf[group, place] = passed
+                    high_buf[group, chunks + place] = own
+                    if place == chunks - 1:
+                        high_copy(group).start()
+            if t == 0:
+                low_copy().start()
+
+        def fill_used(part, columns):
+            used_buf[part, columns] = (
+                val_buf[part, columns] + (1.0 - mixing) * v_buf[1, part, columns].astype(f32)
+            ).astype(bf16)
+
+        def fill_attended(t, heads):
+            part = half_part(t)
+            keys = (t + 1) * half
+            for n in heads:
+                att_buf[part, head_part(n)] = project(
+                    p_buf[n, part, :keys], used_buf[:keys, head_part(n)]
+                ).astype(bf16)
+
+        def finish_rows(t):
+            part = half_part(t)
+            keys = (t + 1) * half
+            for n in range(HEADS):
+                p_buf[n, part, :keys] = probabilities(part, keys, n).astype(bf16)
+            fill_used(part, early)
+            fill_attended(t, range(HEADS - 2))
+            out_acc[part, :] = h_in[1, part, :].astype(f32) + project(att_buf[part, early], wo[early, :])
+
+        val_buf[half_part(0), :] = fill_rows(1, 0)
+        with jax.named_scope("first0"):
+            v_copy(early, 0).wait_recv()
+        finish_rows(0)
+        squares = jnp.zeros((half, 1), f32)
+        for c in range(CUTS):
+            with jax.named_scope(f"cut{c}"):
+                cut_copy(c).wait_recv()
+            arrived = h_in[1, half_part(1), cut_part(c)]
+            for target, weight in ((q_acc, wq), (k_acc, wk), (v_acc, wv)):
+                term = project(arrived, weight[cut_part(c), :])
+                if c == 0:
+                    target[...] = term
+                else:
+                    target[...] += term
+            wide = arrived.astype(f32)
+            squares += jnp.sum(wide * wide, axis=-1, keepdims=True)
+        with jax.named_scope("last"):
+            scale = lax.rsqrt(squares / width + epsilon)
+            fill_heads(q_buf, half_part(1), q_acc[...] * scale)
+            fill_heads(k_buf, half_part(1), k_acc[...] * scale)
+            val_buf[half_part(1), :] = mixing * (v_acc[...] * scale)
+            finish_rows(1)
+        with jax.named_scope("first1"):
+            v_copy(late, 1).wait_recv()
+        with jax.named_scope("out"):
+            fill_used(everything, late)
+            for t in range(2):
+                fill_attended(t, range(HEADS - 2, HEADS))
+            out_ref[0] = (out_acc[...] + project(att_buf[:, late], wo[late, :])).astype(bf16)
+        with jax.named_scope("end"):
+            rows_wait(share - piece, 1, 0).wait_send()
+            send(low_buf, low_buf, 2, 0, {"section": 0}).wait_send()
+            send(high_buf, high_buf, 3, 0, {"section": 0}).wait_send()
+
+
+def pair_body(inputs, w_query, w_key, w_value, w_out, mixing):
+    micro, rows, width = inputs.shape
+    features = w_value.shape[2]
+    half = rows // 2
+    chunks = HEADS // 2
+    head = features // HEADS
+    bf16 = jnp.bfloat16
+    f32 = jnp.float32
+    anywhere = pl.BlockSpec(memory_space=pltpu.HBM)
+    dma = pltpu.SemaphoreType.DMA
+    return pl.pallas_call(
+        pair_kernel,
+        out_shape=pltpu.VMEM((1, rows, width), bf16),
+        in_specs=[anywhere] * 5 + [pl.BlockSpec(memory_space=pltpu.SMEM)],
+        out_specs=pl.BlockSpec(memory_space=pltpu.VMEM),
+        scratch_shapes=[
+            pltpu.VMEM((width, features), bf16),
+            pltpu.VMEM((width, features), bf16),
+            pltpu.VMEM((width, features), bf16),
+            pltpu.VMEM((features, width), bf16),
+            pltpu.VMEM((features, width), bf16),
+            pltpu.VMEM((micro, rows, width), bf16),
+            pltpu.VMEM((micro, rows, width), bf16),
+            pltpu.VMEM((micro * rows, width), bf16),
+            pltpu.VMEM((micro, rows, features), bf16),
+            pltpu.VMEM((rows, features), bf16),
+            pltpu.VMEM((rows, features), bf16),
+            pltpu.VMEM((rows, features), bf16),
+            pltpu.VMEM((HEADS, rows, rows), bf16),
+            pltpu.VMEM((chunks + HEADS, half, head), bf16),
+            pltpu.VMEM((2, HEADS, half, head), bf16),
+            pltpu.VMEM((rows, features), bf16),
+            pltpu.VMEM((half, features), f32),
+            pltpu.VMEM((half, features), f32),
+            pltpu.VMEM((half, features), f32),
+            pltpu.VMEM((rows, features), f32),
+            pltpu.VMEM((rows, width), f32),
+            dma((8,)),
+            dma((4,)),
+            dma((max(5 + CUTS, 4 + 2 * PIECES),)),
+            pltpu.SemaphoreType.REGULAR,
+        ],
+        compiler_params=pltpu.CompilerParams(
+            collective_id=0, has_side_effects=True, vmem_limit_bytes=62 * 1024 * 1024
+        ),
+        name="section_pair",
+    )(inputs, w_query, w_key, w_value, w_out, mixing)
+
+
 def solution(mesh):
     in_specs = (
         P("dp", None, None),
@@ -342,4 +803,11 @@
         P("section"),
     )
     out_specs = P(("dp", "section"), None, None)
-    return jax.shard_map(body, mesh=mesh, in_specs=in_specs, out_specs=out_specs, check_vma=False)
+    paired = mesh.shape["section"] == 2 and mesh.shape["dp"] % 8 == 0
+
+    def either(inputs, *weights):
+        square = inputs.shape[1] * HEADS == weights[2].shape[2]
+        chosen = pair_body if paired and square and inputs.shape[0] == 2 else body
+        return chosen(inputs, *weights)
+
+    return jax.shard_map(either, mesh=mesh, in_specs=in_specs, out_specs=out_specs, check_vma=False)

time: 31.7 us -> 27.4 us (0.86); the launches traced: 31.2 us -> 27.3 us
  Pallas kernels: 29.7 us -> 25.9 us
    pallas_call x1, Pallas kernels: 29.7 us -> 25.9 us  [pair_body(): pl.pallas_call(pair_kernel, out_shape=pltpu.VMEM((1, rows, width), bf16),...]
where the time goes in v2:
time: 27.4 us; the launch traced here: 27.3 us
  Pallas kernels  25.9 us (95%)
  local copies, waits for them, and re-layouts  0.75 us (3%)
  between operations  0.66 us (2%)
    pallas_call x1, Pallas kernels, pair_body(): pl.pallas_call(pair_kernel, out_shape=pltpu.VMEM((1, rows, width), bf16),...  25.9 us
    unnamed x1, local copies, waits for them, and re-layouts  0.75 us

profile of v2, /device:TPU:28, one launch (start us, length us, event | category | flops | bytes accessed | tf_op | source)
XLA Modules:
  0.0 27.3 jit_solution(411086338354547654)
XLA Ops:
  0.7 25.9 %section_pair.1 = bf16[1,128,1536]{2,1,0:T(8,128)(2,1)S(1)} custom-call(bf16[2,128,1536]{2,1,0:T(8,128)(2,1)} %inputs_ref.1, bf16[1,1536,768]{2,1,0:T(8,128)(2,1)} %wq_hbm.1, bf16[1,1536,768]{2,1,0:T(8,128)(2,1)} %wk_hbm.1, bf16[1,1536,768]{2,1,0:T(8,128)(2,1)} %wv_hbm.1, bf16[1,768,1536]{2,1,0:T(8,128)(2,1)} %wo_hbm.1, f32[1]{0:T(128)S(6)} %copy.9.mixing_ref), custom_call_target="tpu_custom_call" | custom-call | tf_op jit(solution)/shard_map/section_pair/pallas_call | solution.py:757
  26.5 0.7 %copy.8 = bf16[1,128,1536]{2,1,0:T(8,128)(2,1)} copy(bf16[1,128,1536]{2,1,0:T(8,128)(2,1)S(1)} %section_pair.1) | data formatting | bytes 786432

commit v3 on v2

--- a/solution.py
+++ b/solution.py
@@ -8,8 +8,9 @@
 from jax.sharding import PartitionSpec as P
 
 HEADS = 6
-CUTS = 6
-PIECES = 4
+CUTS = ((3, 3), (3, 6))
+PIECES = (3, 5)
+HELD = 4
 
 epsilon = 1e-06
 score_scale = 0.12
@@ -374,17 +375,16 @@
     across = dp + 2 - 4 * ((dp // 2) % 2)
     along = dp + 4 - 8 * ((dp // 4) % 2)
     beside = dp + 1 - 2 * core
-    quarter = (dp // 2 + dp // 4) % 2 * 2 + core
-    far_quarter = quarter + 2 - 4 * (quarter // 2)
+    near = (dp // 2 + dp // 4) % 2
+    most = max(PIECES)
     micro, rows, width = h_in.shape
     features = wv.shape[1]
     head = features // HEADS
     chunks = HEADS // 2
     span = features // chunks
     half = rows // 2
-    cut = width // CUTS
-    share = features // 4
-    piece = share // PIECES
+    share = features // 2
+    piece = share // sum(PIECES)
     bf16 = jnp.bfloat16
     f32 = jnp.float32
     everything = slice(0, rows)
@@ -397,8 +397,9 @@
     def chunk_part(j):
         return slice(j * span, (j + 1) * span)
 
-    def cut_part(c):
-        return slice(c * cut, (c + 1) * cut)
+    def cut_parts(i, t):
+        cut = width // CUTS[i][t]
+        return [slice(c * cut, (c + 1) * cut) for c in range(CUTS[i][t])]
 
     def half_part(t):
         return slice(t * half, (t + 1) * half)
@@ -419,11 +420,10 @@
     key_load = load(wk_hbm.at[0], wk, 6)
     out_load = load(wo_hbm.at[0], wo, 7)
     values_load = load(wv_hbm.at[0], wv, 2)
-    rest_load = load(wo_hbm.at[0, : 3 * share, :], wo.at[: 3 * share, :], 1)
 
     def share_load(r):
-        part = pl.ds(pl.multiple_of((quarter + r) % 4 * share, share), share)
-        return load(wo_hbm.at[0, part, :], wo.at[part, :], min(r, 1))
+        part = pl.ds(pl.multiple_of((near + r) % 2 * share, share), share)
+        return load(wo_hbm.at[0, part, :], wo.at[part, :], r)
 
     def send(source, target, sent, received, device):
         return pltpu.make_async_remote_copy(
@@ -435,16 +435,13 @@
             device_id_type=MESH,
         )
 
-    def half_copy(i, t):
-        part = (i, half_part(t))
-        return send(h_out.at[part], h_in.at[part], 0, 2 * i + t, {"section": 1})
-
-    def cut_copy(c):
-        part = (1, half_part(1), cut_part(c))
-        return send(h_out.at[part], h_in.at[part], 0, 3 + c, {"section": 1})
+    def cut_copy(i, t, c):
+        part = (i, half_part(t), cut_parts(i, t)[c])
+        place = sum((CUTS[0] + CUTS[1])[: 2 * i + t]) + c
+        return send(h_out.at[part], h_in.at[part], 0, place, {"section": 1})
 
     def v_copy(part, n):
-        return send(v_buf.at[1, :, part], v_buf.at[1, :, part], 1, 3 + CUTS + n, {"section": 1})
+        return send(v_buf.at[1, :, part], v_buf.at[1, :, part], 1, sum(CUTS[0] + CUTS[1]) + n, {"section": 1})
 
     def low_copy():
         return send(low_buf, low_buf, 2, 0, {"section": 0})
@@ -452,24 +449,35 @@
     def high_copy(g):
         return send(high_buf.at[g], high_buf.at[g], 3, 1 + g, {"section": 0})
 
-    def piece_part(owner, i):
-        return pl.ds(pl.multiple_of(owner * share + i * piece, piece), piece)
+    def piece_part(far, i):
+        start = (near + far) % 2 * share + core * PIECES[0] * piece + i * piece
+        return pl.ds(pl.multiple_of(start, piece), piece)
 
     def y_copy(i):
-        part = piece_part(quarter, i)
+        part = piece_part(0, i)
         return send(wo.at[part, :], wx.at[part, :], min(i, 1), 3 + i, {"section": 0})
 
-    def side_copy(owner, i):
-        part = wx.at[piece_part(owner, i), :]
-        return send(part, part, 2, 3 + PIECES + i, {"dp": along if i % 2 else across})
-
-    def core_copy(owner, i):
-        part = wx.at[piece_part(owner, i), :]
-        return send(part, part, 3, 3 + 2 * PIECES, {"dp": beside})
-
-    def rows_wait(count, sent, received):
-        part = wx.at[:count, :]
+    def side_copy(far, i):
+        part = wx.at[piece_part(far, i), :]
+        return send(part, part, 2, 3 + most + i, {"dp": along if i % 2 else across})
+
+    def core_copy(far, i):
+        part = wx.at[piece_part(far, i), :]
+        return send(part, part, 3, 3 + 2 * most, {"dp": beside})
+
+    def pieces_wait(count, sent, received):
+        part = wx.at[: count * piece, :]
         return send(part, part, sent, received, {"dp": beside})
+
+    def for_piece(i, run):
+        if i < min(PIECES):
+            run()
+        else:
+            pl.when(core == 1)(run)
+
+    def for_core(run):
+        for n in range(2):
+            pl.when(core == n)(functools.partial(run, PIECES[n], PIECES[1 - n]))
 
     barrier = pltpu.get_barrier_semaphore()
 
@@ -530,26 +538,20 @@
         query_load.start()
         key_load.start()
         out_load.start()
-        for j in range(chunks):
+        for j in range(chunks - 1):
             with jax.named_scope(f"wv{j}"):
                 value_load(j).wait()
             fill_values(1, j)
             if j == 0:
                 with jax.named_scope("met"):
                     pl.semaphore_wait(met_sem, 1)
-            if j < chunks - 1:
-                v_copy(chunk_part(j), 0).start()
-            else:
-
-                @pl.when(core == 0)
-                def _():
-                    v_copy(late, 1).start()
-
+            v_copy(chunk_part(j), 0).start()
         fill_normed(0)
+        value_load(chunks - 1).wait()
         for j in range(chunks):
             fill_values(0, j)
 
-        def attend(i):
+        def fill_queries(i):
             normed = normed_buf[sequence_part(i), :]
             if i == 0:
                 with jax.named_scope("wq"):
@@ -559,55 +561,69 @@
                 with jax.named_scope("wk"):
                     key_load.wait()
             fill_heads(k_buf, everything, project(normed, wk[...]))
+
+        def attend(i, part, keys):
             for n in range(HEADS):
-                p_buf[n] = probabilities(everything, rows, n).astype(bf16)
+                p_buf[n, part, :keys] = probabilities(part, keys, n).astype(bf16)
             for n in range(HEADS):
-                att_buf[:, head_part(n)] = project(p_buf[n], v_buf[i, :, head_part(n)]).astype(bf16)
-
-        def next_rows(i, part, columns):
-            h_out[i, part, columns] = (
-                h_in[i, part, columns].astype(f32) + project(att_buf[part, :], wo[:, columns])
-            ).astype(bf16)
+                att_buf[part, head_part(n)] = project(
+                    p_buf[n, part, :keys], v_buf[i, :keys, head_part(n)]
+                ).astype(bf16)
+
+        def next_rows(i, t):
+            part = half_part(t)
+            for c, columns in enumerate(cut_parts(i, t)):
+                h_out[i, part, columns] = (
+                    h_in[i, part, columns].astype(f32) + project(att_buf[part, :], wo[:, columns])
+                ).astype(bf16)
+                if (i, t) == (0, 0) or (i, t) == (1, 1) and c > HELD:
+                    cut_copy(i, t, c).start()
+                if (i, t, c) == (1, 1, HELD):
+                    pl.when(core == 1)(functools.partial(start_rows, 0, 1))
+                    start_rows(1, 0)
+                    for earlier in range(c + 1):
+                        cut_copy(i, t, earlier).start()
+
+        def start_rows(i, t):
+            for c in range(CUTS[i][t]):
+                cut_copy(i, t, c).start()
 
         def pass_on(i):
             with jax.named_scope(f"pass{i}"):
                 y_copy(i).wait_recv()
-            side_copy(quarter, i).start()
-            core_copy(quarter, i).start()
+            side_copy(0, i).start()
+            core_copy(0, i).start()
 
         def pass_far(i):
             with jax.named_scope(f"far{i}"):
-                side_copy(far_quarter, i).wait_recv()
-            core_copy(far_quarter, i).start()
-
-        attend(0)
-        with jax.named_scope("wo"):
-            out_load.wait()
+                side_copy(1, i).wait_recv()
+            core_copy(1, i).start()
+
+        fill_queries(0)
         for t in range(2):
+            attend(0, half_part(t), (t + 1) * half)
+            if t == 0:
+                with jax.named_scope("wo"):
+                    out_load.wait()
             with jax.named_scope(f"h0{t}"):
-                next_rows(0, half_part(t), slice(0, width))
-                half_copy(0, t).start()
+                next_rows(0, t)
+        pl.when(core == 0)(functools.partial(start_rows, 0, 1))
+        fill_values(1, chunks - 1)
         with jax.named_scope("bar"):
             pl.semaphore_wait(barrier, 3)
         pass_on(0)
-        attend(1)
+        fill_queries(1)
+        attend(1, everything, rows)
         with jax.named_scope("h1"):
-            next_rows(1, half_part(0), slice(0, width))
-            half_copy(1, 0).start()
-            for c in range(CUTS):
-                next_rows(1, half_part(1), cut_part(c))
-                cut_copy(c).start()
-
-        @pl.when(core == 1)
-        def _():
-            v_copy(late, 1).start()
-
-        for i in range(1, PIECES):
-            pass_on(i)
-            pass_far(i - 1)
-        pass_far(PIECES - 1)
+            for t in range(2):
+                next_rows(1, t)
+        v_copy(late, 1).start()
+        for i in range(1, most):
+            for_piece(i, functools.partial(pass_on, i))
+            for_piece(i - 1, functools.partial(pass_far, i - 1))
+        for_piece(most - 1, functools.partial(pass_far, most - 1))
         with jax.named_scope("core"):
-            rows_wait(2 * share, 3, 3 + 2 * PIECES).wait_recv()
+            for_core(lambda own, other: pieces_wait(2 * other, 3, 3 + 2 * most).wait_recv())
         for t in range(2):
             part = half_part(t)
             keys = (t + 1) * half
@@ -634,37 +650,47 @@
         with jax.named_scope("end"):
             send(h_out, h_in, 0, 0, {"section": 1}).wait_send()
             send(v_buf.at[1], v_buf.at[1], 1, 0, {"section": 1}).wait_send()
-            rows_wait(share, 2, 0).wait_send()
-            rows_wait(2 * share, 3, 0).wait_send()
+            for_core(lambda own, other: pieces_wait(own, 2, 0).wait_send())
+            for_core(lambda own, other: pieces_wait(2 * own, 3, 0).wait_send())
 
     @pl.when(me == 1)
     def _():
         mixing = mixing_ref[0]
         with jax.named_scope("wo"):
             share_load(0).wait()
-        for i in range(PIECES):
-            y_copy(i).start()
+        for i in range(most):
+            for_piece(i, lambda: y_copy(i).start())
         with jax.named_scope("y0"):
-            rows_wait(piece, 0, 0).wait_send()
+            pieces_wait(1, 0, 0).wait_send()
         query_load.start()
         key_load.start()
         values_load.start()
-        for r in range(1, 4):
-            share_load(r).start()
+        share_load(1).start()
         with jax.named_scope("loads"):
             query_load.wait()
             key_load.wait()
             values_load.wait()
-            rest_load.wait()
+            share_load(1).wait()
 
         def fill_rows(i, t):
             part = half_part(t)
-            with jax.named_scope(f"half{i}{t}"):
-                half_copy(i, t).wait_recv()
-            normed = normed_rows(h_in[i, part, :])
-            fill_heads(q_buf, part, project(normed, wq[...]))
-            fill_heads(k_buf, part, project(normed, wk[...]))
-            return mixing * project(normed, wv[...])
+            squares = jnp.zeros((half, 1), f32)
+            for c, columns in enumerate(cut_parts(i, t)):
+                with jax.named_scope(f"cut{i}{t}{c}"):
+                    cut_copy(i, t, c).wait_recv()
+                arrived = h_in[i, part, columns]
+                for target, weight in ((q_acc, wq), (k_acc, wk), (v_acc, wv)):
+                    term = project(arrived, weight[columns, :])
+                    if c == 0:
+                        target[...] = term
+                    else:
+                        target[...] += term
+                wide = arrived.astype(f32)
+                squares += jnp.sum(wide * wide, axis=-1, keepdims=True)
+            scale = lax.rsqrt(squares / width + epsilon)
+            fill_heads(q_buf, part, q_acc[...] * scale)
+            fill_heads(k_buf, part, k_acc[...] * scale)
+            return mixing * (v_acc[...] * scale)
 
         for t in range(2):
             part = half_part(t)
@@ -706,32 +732,17 @@
                 p_buf[n, part, :keys] = probabilities(part, keys, n).astype(bf16)
             fill_used(part, early)
             fill_attended(t, range(HEADS - 2))
-            out_acc[part, :] = h_in[1, part, :].astype(f32) + project(att_buf[part, early], wo[early, :])
+            out_acc[part, :] = h_in[1, part, :].astype(f32) + project(
+                att_buf[part, early], wo[early, :]
+            )
 
         val_buf[half_part(0), :] = fill_rows(1, 0)
-        with jax.named_scope("first0"):
-            v_copy(early, 0).wait_recv()
+        v_copy(early, 0).wait_recv()
         finish_rows(0)
-        squares = jnp.zeros((half, 1), f32)
-        for c in range(CUTS):
-            with jax.named_scope(f"cut{c}"):
-                cut_copy(c).wait_recv()
-            arrived = h_in[1, half_part(1), cut_part(c)]
-            for target, weight in ((q_acc, wq), (k_acc, wk), (v_acc, wv)):
-                term = project(arrived, weight[cut_part(c), :])
-                if c == 0:
-                    target[...] = term
-                else:
-                    target[...] += term
-            wide = arrived.astype(f32)
-            squares += jnp.sum(wide * wide, axis=-1, keepdims=True)
+        val_buf[half_part(1), :] = fill_rows(1, 1)
         with jax.named_scope("last"):
-            scale = lax.rsqrt(squares / width + epsilon)
-            fill_heads(q_buf, half_part(1), q_acc[...] * scale)
-            fill_heads(k_buf, half_part(1), k_acc[...] * scale)
-            val_buf[half_part(1), :] = mixing * (v_acc[...] * scale)
             finish_rows(1)
-        with jax.named_scope("first1"):
+        with jax.named_scope("first"):
             v_copy(late, 1).wait_recv()
         with jax.named_scope("out"):
             fill_used(everything, late)
@@ -739,7 +750,7 @@
                 fill_attended(t, range(HEADS - 2, HEADS))
             out_ref[0] = (out_acc[...] + project(att_buf[:, late], wo[late, :])).astype(bf16)
         with jax.named_scope("end"):
-            rows_wait(share - piece, 1, 0).wait_send()
+            for_core(lambda own, other: pieces_wait(own - 1, 1, 0).wait_send())
             send(low_buf, low_buf, 2, 0, {"section": 0}).wait_send()
             send(high_buf, high_buf, 3, 0, {"section": 0}).wait_send()
 
@@ -783,7 +794,7 @@
             pltpu.VMEM((rows, width), f32),
             dma((8,)),
             dma((4,)),
-            dma((max(5 + CUTS, 4 + 2 * PIECES),)),
+            dma((max(2 + sum(CUTS[0] + CUTS[1]), 4 + 2 * max(PIECES)),)),
             pltpu.SemaphoreType.REGULAR,
         ],
         compiler_params=pltpu.CompilerParams(

time: 27.4 us -> 26.9 us (0.982); the launches traced: 27.3 us -> 26.5 us
  Pallas kernels: 25.9 us -> 25.1 us
    pallas_call x1, Pallas kernels: 25.9 us -> 25.1 us  [pair_body(): pl.pallas_call(pair_kernel, out_shape=pltpu.VMEM((1, rows, width), bf16),...]
where the time goes in v3:
time: 26.9 us; the launch traced here: 26.5 us
  Pallas kernels  25.1 us (93%)
  local copies, waits for them, and re-layouts  0.75 us (3%)
  between operations  0.66 us (2%)
    pallas_call x1, Pallas kernels, pair_body(): pl.pallas_call(pair_kernel, out_shape=pltpu.VMEM((1, rows, width), bf16),...  25.1 us
    unnamed x1, local copies, waits for them, and re-layouts  0.75 us

profile of v3, /device:TPU:28, one launch (start us, length us, event | category | flops | bytes accessed | tf_op | source)
XLA Modules:
  0.0 26.5 jit_solution(16535431236113076067)
XLA Ops:
  0.7 25.1 %section_pair.1 = bf16[1,128,1536]{2,1,0:T(8,128)(2,1)S(1)} custom-call(bf16[2,128,1536]{2,1,0:T(8,128)(2,1)} %inputs_ref.1, bf16[1,1536,768]{2,1,0:T(8,128)(2,1)} %wq_hbm.1, bf16[1,1536,768]{2,1,0:T(8,128)(2,1)} %wk_hbm.1, bf16[1,1536,768]{2,1,0:T(8,128)(2,1)} %wv_hbm.1, bf16[1,768,1536]{2,1,0:T(8,128)(2,1)} %wo_hbm.1, f32[1]{0:T(128)S(6)} %copy.9.mixing_ref), custom_call_target="tpu_custom_call" | custom-call | tf_op jit(solution)/shard_map/section_pair/pallas_call | solution.py:768
  25.7 0.7 %copy.8 = bf16[1,128,1536]{2,1,0:T(8,128)(2,1)} copy(bf16[1,128,1536]{2,1,0:T(8,128)(2,1)S(1)} %section_pair.1) | data formatting | bytes 786432

commit v4 on v3

--- a/solution.py
+++ b/solution.py
@@ -8,9 +8,10 @@
 from jax.sharding import PartitionSpec as P
 
 HEADS = 6
-CUTS = ((3, 3), (3, 6))
+THIRDS = (0, 4, 8, 12)
+CUTS = ((THIRDS, THIRDS), (THIRDS, (0, 4, 8, 10, 11, 12)))
+COUNTS = [len(CUTS[n // 2][n % 2]) - 1 for n in range(4)]
 PIECES = (3, 5)
-HELD = 4
 
 epsilon = 1e-06
 score_scale = 0.12
@@ -377,6 +378,8 @@
     beside = dp + 1 - 2 * core
     near = (dp // 2 + dp // 4) % 2
     most = max(PIECES)
+    column = dp // 2 % 2
+    mine, missed = most - 1 - column, most - 2 + column
     micro, rows, width = h_in.shape
     features = wv.shape[1]
     head = features // HEADS
@@ -398,8 +401,8 @@
         return slice(j * span, (j + 1) * span)
 
     def cut_parts(i, t):
-        cut = width // CUTS[i][t]
-        return [slice(c * cut, (c + 1) * cut) for c in range(CUTS[i][t])]
+        ends = [width * n // 12 for n in CUTS[i][t]]
+        return [slice(*pair) for pair in zip(ends, ends[1:])]
 
     def half_part(t):
         return slice(t * half, (t + 1) * half)
@@ -437,11 +440,11 @@
 
     def cut_copy(i, t, c):
         part = (i, half_part(t), cut_parts(i, t)[c])
-        place = sum((CUTS[0] + CUTS[1])[: 2 * i + t]) + c
-        return send(h_out.at[part], h_in.at[part], 0, place, {"section": 1})
+        place = sum(COUNTS[: 2 * i + t]) + c
+        return send(h_out.at[part], h_in.at[part], 0 if i or t else 4, place, {"section": 1})
 
     def v_copy(part, n):
-        return send(v_buf.at[1, :, part], v_buf.at[1, :, part], 1, sum(CUTS[0] + CUTS[1]) + n, {"section": 1})
+        return send(v_buf.at[1, :, part], v_buf.at[1, :, part], 1, sum(COUNTS) + n, {"section": 1})
 
     def low_copy():
         return send(low_buf, low_buf, 2, 0, {"section": 0})
@@ -455,12 +458,25 @@
 
     def y_copy(i):
         part = piece_part(0, i)
-        return send(wo.at[part, :], wx.at[part, :], min(i, 1), 3 + i, {"section": 0})
+        sent = 1 if i else core
+        return send(wo.at[part, :], wx.at[part, :], sent, 3 + i, {"section": 0})
 
     def side_copy(far, i):
         part = wx.at[piece_part(far, i), :]
         return send(part, part, 2, 3 + most + i, {"dp": along if i % 2 else across})
 
+    def rare_copy():
+        part = piece_part(0, mine)
+        return send(wo.at[part, :], wx.at[part, :], 0, 1 + most, {"section": 0})
+
+    def rare_side(step):
+        part = wx.at[piece_part(0, mine), :]
+        return send(part, part, 2, 1 + 2 * most + step, {"dp": across if step else along})
+
+    def relay_copy():
+        part = wx.at[piece_part(1, missed), :]
+        return send(part, part, 2, 2 + most, {"dp": along})
+
     def core_copy(far, i):
         part = wx.at[piece_part(far, i), :]
         return send(part, part, 3, 3 + 2 * most, {"dp": beside})
@@ -469,11 +485,9 @@
         part = wx.at[: count * piece, :]
         return send(part, part, sent, received, {"dp": beside})
 
-    def for_piece(i, run):
-        if i < min(PIECES):
-            run()
-        else:
-            pl.when(core == 1)(run)
+    def rows_sent(count, sent):
+        part = wx.at[:count, :]
+        return send(part, part, sent, 0, {"section": 1})
 
     def for_core(run):
         for n in range(2):
@@ -546,8 +560,14 @@
                 with jax.named_scope("met"):
                     pl.semaphore_wait(met_sem, 1)
             v_copy(chunk_part(j), 0).start()
+        value_load(chunks - 1).wait()
+
+        @pl.when(core == 0)
+        def _():
+            fill_values(1, chunks - 1)
+            v_copy(late, 1).start()
+
         fill_normed(0)
-        value_load(chunks - 1).wait()
         for j in range(chunks):
             fill_values(0, j)
 
@@ -576,16 +596,11 @@
                 h_out[i, part, columns] = (
                     h_in[i, part, columns].astype(f32) + project(att_buf[part, :], wo[:, columns])
                 ).astype(bf16)
-                if (i, t) == (0, 0) or (i, t) == (1, 1) and c > HELD:
+                if (i, t) == (0, 0):
                     cut_copy(i, t, c).start()
-                if (i, t, c) == (1, 1, HELD):
-                    pl.when(core == 1)(functools.partial(start_rows, 0, 1))
-                    start_rows(1, 0)
-                    for earlier in range(c + 1):
-                        cut_copy(i, t, earlier).start()
 
         def start_rows(i, t):
-            for c in range(CUTS[i][t]):
+            for c in range(COUNTS[2 * i + t]):
                 cut_copy(i, t, c).start()
 
         def pass_on(i):
@@ -608,20 +623,60 @@
             with jax.named_scope(f"h0{t}"):
                 next_rows(0, t)
         pl.when(core == 0)(functools.partial(start_rows, 0, 1))
-        fill_values(1, chunks - 1)
+        pl.when(core == 1)(functools.partial(fill_values, 1, chunks - 1))
         with jax.named_scope("bar"):
             pl.semaphore_wait(barrier, 3)
-        pass_on(0)
+
+        @pl.when(core == 1)
+        def _():
+            with jax.named_scope("rare"):
+                rare_copy().wait_recv()
+            for step in range(2):
+                rare_side(step).start()
+            core_copy(0, mine).start()
+
+        pl.when(core == 0)(functools.partial(pass_on, 0))
         fill_queries(1)
         attend(1, everything, rows)
         with jax.named_scope("h1"):
             for t in range(2):
                 next_rows(1, t)
-        v_copy(late, 1).start()
-        for i in range(1, most):
-            for_piece(i, functools.partial(pass_on, i))
-            for_piece(i - 1, functools.partial(pass_far, i - 1))
-        for_piece(most - 1, functools.partial(pass_far, most - 1))
+                pl.when(core == 0)(functools.partial(start_rows, 1, t))
+
+        @pl.when(core == 1)
+        def _():
+            with jax.named_scope("yield"):
+                rows_sent(half, 4).wait_send()
+            start_rows(0, 1)
+            for t in range(2):
+                start_rows(1, t)
+
+        pl.when(core == 1)(lambda: v_copy(late, 1).start())
+        pl.when(core == 1)(functools.partial(pass_on, 0))
+        pass_on(1)
+
+        @pl.when(core == 1)
+        def _():
+            with jax.named_scope("across"):
+                rare_side(1).wait_recv()
+            relay_copy().start()
+            core_copy(1, missed).start()
+            with jax.named_scope("along"):
+                rare_side(0).wait_recv()
+            core_copy(1, mine).start()
+
+        pass_far(0)
+        for i in range(2, min(PIECES)):
+            pass_on(i)
+            pass_far(i - 1)
+
+        @pl.when(core == 1)
+        def _():
+            with jax.named_scope("relay"):
+                relay_copy().wait_recv()
+            core_copy(0, missed).start()
+
+        pass_far(min(PIECES) - 1)
         with jax.named_scope("core"):
             for_core(lambda own, other: pieces_wait(2 * other, 3, 3 + 2 * most).wait_recv())
         for t in range(2):
@@ -648,9 +703,10 @@
                 h_out[0, part, :].astype(f32) + project(att_buf[part, :], wx[...])
             ).astype(bf16)
         with jax.named_scope("end"):
-            send(h_out, h_in, 0, 0, {"section": 1}).wait_send()
+            pl.when(core == 0)(rows_sent(half, 4).wait_send)
+            rows_sent(3 * half, 0).wait_send()
             send(v_buf.at[1], v_buf.at[1], 1, 0, {"section": 1}).wait_send()
-            for_core(lambda own, other: pieces_wait(own, 2, 0).wait_send())
+            for_core(lambda own, other: pieces_wait(own + own // most, 2, 0).wait_send())
             for_core(lambda own, other: pieces_wait(2 * own, 3, 0).wait_send())
 
     @pl.when(me == 1)
@@ -658,8 +714,9 @@
         mixing = mixing_ref[0]
         with jax.named_scope("wo"):
             share_load(0).wait()
-        for i in range(most):
-            for_piece(i, lambda: y_copy(i).start())
+        pl.when(core == 1)(lambda: rare_copy().start())
+        for i in range(min(PIECES)):
+            y_copy(i).start()
         with jax.named_scope("y0"):
             pieces_wait(1, 0, 0).wait_send()
         query_load.start()
@@ -725,32 +782,45 @@
                     p_buf[n, part, :keys], used_buf[:keys, head_part(n)]
                 ).astype(bf16)
 
-        def finish_rows(t):
+        def finish_rows(t, columns):
             part = half_part(t)
             keys = (t + 1) * half
             for n in range(HEADS):
                 p_buf[n, part, :keys] = probabilities(part, keys, n).astype(bf16)
-            fill_used(part, early)
-            fill_attended(t, range(HEADS - 2))
-            out_acc[part, :] = h_in[1, part, :].astype(f32) + project(
-                att_buf[part, early], wo[early, :]
-            )
+            fill_used(part, columns)
+            fill_attended(t, range(columns.stop // head))
+            return h_in[1, part, :].astype(f32) + project(att_buf[part, columns], wo[columns, :])
+
+        def finish_either(t):
+            @pl.when(core == 0)
+            def _():
+                if t == 0:
+                    v_copy(late, 1).wait_recv()
+                out_ref[0, half_part(t), :] = finish_rows(t, slice(0, features)).astype(bf16)
+
+            @pl.when(core == 1)
+            def _():
+                out_acc[half_part(t), :] = finish_rows(t, early)
 
         val_buf[half_part(0), :] = fill_rows(1, 0)
         v_copy(early, 0).wait_recv()
-        finish_rows(0)
+        finish_either(0)
         val_buf[half_part(1), :] = fill_rows(1, 1)
         with jax.named_scope("last"):
-            finish_rows(1)
-        with jax.named_scope("first"):
-            v_copy(late, 1).wait_recv()
-        with jax.named_scope("out"):
-            fill_used(everything, late)
-            for t in range(2):
-                fill_attended(t, range(HEADS - 2, HEADS))
-            out_ref[0] = (out_acc[...] + project(att_buf[:, late], wo[late, :])).astype(bf16)
+            finish_either(1)
+
+        @pl.when(core == 1)
+        def _():
+            with jax.named_scope("first"):
+                v_copy(late, 1).wait_recv()
+            with jax.named_scope("out"):
+                fill_used(everything, late)
+                for t in range(2):
+                    fill_attended(t, range(HEADS - 2, HEADS))
+                out_ref[0] = (out_acc[...] + project(att_buf[:, late], wo[late, :])).astype(bf16)
+
         with jax.named_scope("end"):
-            for_core(lambda own, other: pieces_wait(own - 1, 1, 0).wait_send())
+            for_core(lambda own, other: pieces_wait(own - 1 - own // most, 1, 0).wait_send())
             send(low_buf, low_buf, 2, 0, {"section": 0}).wait_send()
             send(high_buf, high_buf, 3, 0, {"section": 0}).wait_send()
 
@@ -793,8 +863,8 @@
             pltpu.VMEM((rows, features), f32),
             pltpu.VMEM((rows, width), f32),
             dma((8,)),
-            dma((4,)),
-            dma((max(2 + sum(CUTS[0] + CUTS[1]), 4 + 2 * max(PIECES)),)),
+            dma((5,)),
+            dma((max(2 + sum(COUNTS), 4 + 2 * max(PIECES)),)),
             pltpu.SemaphoreType.REGULAR,
         ],
         compiler_params=pltpu.CompilerParams(

time: 26.9 us -> 26.6 us (0.989); the launches traced: 26.5 us -> 26.5 us
  no operation moved by 1% of the time
where the time goes in v4:
time: 26.6 us; the launch traced here: 26.5 us
  Pallas kernels  25.1 us (94%)
  local copies, waits for them, and re-layouts  0.75 us (3%)
  between operations  0.66 us (2%)
    pallas_call x1, Pallas kernels, pair_body(): pl.pallas_call(pair_kernel, out_shape=pltpu.VMEM((1, rows, width), bf16),...  25.1 us
    unnamed x1, local copies, waits for them, and re-layouts  0.75 us

profile of v4, /device:TPU:28, one launch (start us, length us, event | category | flops | bytes accessed | tf_op | source)
XLA Modules:
  0.0 26.5 jit_solution(16723672598822098140)
XLA Ops:
  0.7 25.1 %section_pair.1 = bf16[1,128,1536]{2,1,0:T(8,128)(2,1)S(1)} custom-call(bf16[2,128,1536]{2,1,0:T(8,128)(2,1)} %inputs_ref.1, bf16[1,1536,768]{2,1,0:T(8,128)(2,1)} %wq_hbm.1, bf16[1,1536,768]{2,1,0:T(8,128)(2,1)} %wk_hbm.1, bf16[1,1536,768]{2,1,0:T(8,128)(2,1)} %wv_hbm.1, bf16[1,768,1536]{2,1,0:T(8,128)(2,1)} %wo_hbm.1, f32[1]{0:T(128)S(6)} %copy.9.mixing_ref), custom_call_target="tpu_custom_call" | custom-call | tf_op jit(solution)/shard_map/section_pair/pallas_call | solution.py:838
  25.7 0.7 %copy.8 = bf16[1,128,1536]{2,1,0:T(8,128)(2,1)} copy(bf16[1,128,1536]{2,1,0:T(8,128)(2,1)S(1)} %section_pair.1) | data formatting | bytes 786432

commit v5 on v4

--- a/solution.py
+++ b/solution.py
@@ -9,7 +9,8 @@
 
 HEADS = 6
 THIRDS = (0, 4, 8, 12)
-CUTS = ((THIRDS, THIRDS), (THIRDS, (0, 4, 8, 10, 11, 12)))
+HALVES = (0, 6, 12)
+CUTS = ((THIRDS, HALVES), (HALVES, (0, 4, 8, 10, 11, 12)))
 COUNTS = [len(CUTS[n // 2][n % 2]) - 1 for n in range(4)]
 PIECES = (3, 5)
 
@@ -411,22 +412,22 @@
         return slice(i * rows, (i + 1) * rows)
 
     def load(source, target, n):
-        return pltpu.make_async_copy(source, target, load_sem.at[n])
+        return pltpu.make_async_copy(source, target, n)
 
     def input_load(i):
-        return load(inputs_ref.at[i], h_in.at[i], i)
+        return load(inputs_ref.at[i], h_in.at[i], send_sem.at[i])
 
     def value_load(j):
-        return load(wv_hbm.at[0, :, chunk_part(j)], wv.at[:, chunk_part(j)], 2 + j)
-
-    query_load = load(wq_hbm.at[0], wq, 5)
-    key_load = load(wk_hbm.at[0], wk, 6)
-    out_load = load(wo_hbm.at[0], wo, 7)
-    values_load = load(wv_hbm.at[0], wv, 2)
+        return load(wv_hbm.at[0, :, chunk_part(j)], wv.at[:, chunk_part(j)], load_sem.at[j])
+
+    query_load = load(wq_hbm.at[0], wq, send_sem.at[2])
+    key_load = load(wk_hbm.at[0], wk, send_sem.at[3])
+    out_load = load(wo_hbm.at[0], wo, send_sem.at[4])
+    values_load = load(wv_hbm.at[0], wv, load_sem.at[2])
 
     def share_load(r):
         part = pl.ds(pl.multiple_of((near + r) % 2 * share, share), share)
-        return load(wo_hbm.at[0, part, :], wo.at[part, :], r)
+        return load(wo_hbm.at[0, part, :], wo.at[part, :], load_sem.at[r])
 
     def send(source, target, sent, received, device):
         return pltpu.make_async_remote_copy(
@@ -862,7 +863,7 @@
             pltpu.VMEM((half, features), f32),
             pltpu.VMEM((rows, features), f32),
             pltpu.VMEM((rows, width), f32),
-            dma((8,)),
+            dma((3,)),
             dma((5,)),
             dma((max(2 + sum(COUNTS), 4 + 2 * max(PIECES)),)),
             pltpu.SemaphoreType.REGULAR,

time: 26.6 us -> 26.7 us (level)
  no operation moved by 1% of the time
where the time goes in v5:
time: 26.7 us; the launch traced here: 26.6 us
  Pallas kernels  25.1 us (94%)
  local copies, waits for them, and re-layouts  0.75 us (3%)
  between operations  0.66 us (2%)
    pallas_call x1, Pallas kernels, pair_body(): pl.pallas_call(pair_kernel, out_shape=pltpu.VMEM((1, rows, width), bf16),...  25.1 us
    unnamed x1, local copies, waits for them, and re-layouts  0.75 us

profile of v5, /device:TPU:28, one launch (start us, length us, event | category | flops | bytes accessed | tf_op | source)
XLA Modules:
  0.0 26.6 jit_solution(3704761411854435360)
XLA Ops:
  0.7 25.1 %section_pair.1 = bf16[1,128,1536]{2,1,0:T(8,128)(2,1)S(1)} custom-call(bf16[2,128,1536]{2,1,0:T(8,128)(2,1)} %inputs_ref.1, bf16[1,1536,768]{2,1,0:T(8,128)(2,1)} %wq_hbm.1, bf16[1,1536,768]{2,1,0:T(8,128)(2,1)} %wk_hbm.1, bf16[1,1536,768]{2,1,0:T(8,128)(2,1)} %wv_hbm.1, bf16[1,768,1536]{2,1,0:T(8,128)(2,1)} %wo_hbm.1, f32[1]{0:T(128)S(6)} %copy.9.mixing_ref), custom_call_target="tpu_custom_call" | custom-call | tf_op jit(solution)/shard_map/section_pair/pallas_call | solution.py:839
  25.8 0.7 %copy.8 = bf16[1,128,1536]{2,1,0:T(8,128)(2,1)} copy(bf16[1,128,1536]{2,1,0:T(8,128)(2,1)S(1)} %section_pair.1) | data formatting | bytes 786432

commit v6 on v5

--- a/solution.py
+++ b/solution.py
@@ -442,7 +442,7 @@
     def cut_copy(i, t, c):
         part = (i, half_part(t), cut_parts(i, t)[c])
         place = sum(COUNTS[: 2 * i + t]) + c
-        return send(h_out.at[part], h_in.at[part], 0 if i or t else 4, place, {"section": 1})
+        return send(h_out.at[part], h_in.at[part], 0 if i else 4, place, {"section": 1})
 
     def v_copy(part, n):
         return send(v_buf.at[1, :, part], v_buf.at[1, :, part], 1, sum(COUNTS) + n, {"section": 1})
@@ -649,10 +649,7 @@
             with jax.named_scope("yield"):
                 rows_sent(half, 4).wait_send()
             start_rows(0, 1)
-            for t in range(2):
-                start_rows(1, t)
-
-        pl.when(core == 1)(lambda: v_copy(late, 1).start())
+
         pl.when(core == 1)(functools.partial(pass_on, 0))
         pass_on(1)
 
@@ -667,6 +664,15 @@
             core_copy(1, mine).start()
 
         pass_far(0)
+
+        @pl.when(core == 1)
+        def _():
+            with jax.named_scope("yield"):
+                rows_sent(half, 4).wait_send()
+            for t in range(2):
+                start_rows(1, t)
+            v_copy(late, 1).start()
+
         for i in range(2, min(PIECES)):
             pass_on(i)
             pass_far(i - 1)
@@ -704,8 +710,8 @@
                 h_out[0, part, :].astype(f32) + project(att_buf[part, :], wx[...])
             ).astype(bf16)
         with jax.named_scope("end"):
-            pl.when(core == 0)(rows_sent(half, 4).wait_send)
-            rows_sent(3 * half, 0).wait_send()
+            pl.when(core == 0)(rows_sent(rows, 4).wait_send)
+            rows_sent(rows, 0).wait_send()
             send(v_buf.at[1], v_buf.at[1], 1, 0, {"section": 1}).wait_send()
             for_core(lambda own, other: pieces_wait(own + own // most, 2, 0).wait_send())
             for_core(lambda own, other: pieces_wait(2 * own, 3, 0).wait_send())

time: 26.7 us -> 26.9 us (level)
  the two profiles are of different devices: /device:TPU:28 before, /device:TPU:21 now
where the time goes in v6:
time: 26.9 us; the launch traced here: 26.8 us
  Pallas kernels  25.4 us (94%)
  local copies, waits for them, and re-layouts  0.75 us (3%)
  between operations  0.66 us (2%)
    pallas_call x1, Pallas kernels, pair_body(): pl.pallas_call(pair_kernel, out_shape=pltpu.VMEM((1, rows, width), bf16),...  25.4 us
    unnamed x1, local copies, waits for them, and re-layouts  0.75 us

profile of v6, /device:TPU:21, one launch (start us, length us, event | category | flops | bytes accessed | tf_op | source)
XLA Modules:
  0.0 26.8 jit_solution(10820772581780174783)
XLA Ops:
  0.7 25.4 %section_pair.1 = bf16[1,128,1536]{2,1,0:T(8,128)(2,1)S(1)} custom-call(bf16[2,128,1536]{2,1,0:T(8,128)(2,1)} %inputs_ref.1, bf16[1,1536,768]{2,1,0:T(8,128)(2,1)} %wq_hbm.1, bf16[1,1536,768]{2,1,0:T(8,128)(2,1)} %wk_hbm.1, bf16[1,1536,768]{2,1,0:T(8,128)(2,1)} %wv_hbm.1, bf16[1,768,1536]{2,1,0:T(8,128)(2,1)} %wo_hbm.1, f32[1]{0:T(128)S(6)} %copy.9.mixing_ref), custom_call_target="tpu_custom_call" | custom-call | tf_op jit(solution)/shard_map/section_pair/pallas_call | solution.py:845
  26.0 0.7 %copy.8 = bf16[1,128,1536]{2,1,0:T(8,128)(2,1)} copy(bf16[1,128,1536]{2,1,0:T(8,128)(2,1)S(1)} %section_pair.1) | data formatting | bytes 786432
